TPU v7x, 32 devices: a whole 2x2x4 slice. The times are simulated.
32 devices in a mesh: section: 4 (over y, core), dp: 8 (over z, x).
Axes of the slice: x: 2, y: 2, z: 4, core: 2. Of those that a mesh axis runs over, the one named last changes fastest.
Arguments:
- tokens: bfloat16 [64, 6144], P('dp', 'section'), may hold values from -6 to 6
- expert_ids: int32 [64, 2], P('dp'), may hold values from 0 to 7, all different within a row; in each aligned block of 8 rows (0 to 7, 8 to 15, ...) at most 4 rows name the same one
- router: bfloat16 [6144, 8], replicated, may hold values from -0.078125 to 0.078125
- w_up: bfloat16 [8, 6144, 16384], P('dp', None, 'section'), may hold values from -0.078125 to 0.078125
- w_down: bfloat16 [8, 16384, 6144], P('dp', 'section'), may hold values from -0.0625 to 0.0625
- attn_queries: bfloat16 [8, 128, 6144], P('dp', None, 'section'), may hold values from -140 to 140
- attn_keys: bfloat16 [8, 128, 6144], P('dp', None, 'section'), may hold values from -8 to 8
- attn_values: bfloat16 [8, 128, 6144], P('dp', None, 'section'), may hold values from -6 to 6
Outputs:
- mixed: bfloat16 [64, 6144], P('dp', 'section')
- attended: bfloat16 [8, 128, 6144], P('dp', None, 'section')
Inputs may be any that keep to these rules, and one draw needn't show every extreme that they name: `expert_ids`: each row names two different experts; among the 8 rows of one dp index (aligned blocks) no expert is named more than 4 times.
All inputs are finite; a program needn't handle non-finite values.
Results may differ from a plain program's by a relative error of at most 0.005.
Values may be sent and summed in bfloat16 or wider, within the bound.
A program may use at most 192 MiB of HBM per device.

v0:
```python
import math

import jax
import jax.numpy as jnp
from jax import lax
from jax.sharding import PartitionSpec as P

HEAD_DIM = 128
CAP = 4


def route_slots(expert_ids, block_count, per_block, experts):
    pair_ids = expert_ids.reshape(block_count, per_block * 2)
    onehot = (pair_ids[:, :, None] == jnp.arange(experts, dtype=jnp.int32)[None, None, :]).astype(
        jnp.int32
    )
    before = jnp.cumsum(onehot, axis=1) - onehot
    slot_rank = jnp.sum(before * onehot, axis=2)
    return slot_rank.reshape(block_count * per_block, 2)


def attend_head(operands):
    head_queries, head_keys, head_values = operands
    length = head_queries.shape[0]
    scores = jnp.dot(head_queries, head_keys.T, preferred_element_type=jnp.float32) * (
        1.0 / math.sqrt(head_queries.shape[1])
    )
    positions = jnp.arange(length, dtype=jnp.int32)
    causal = positions[None, :] <= positions[:, None]
    scores = jnp.where(causal, scores, -jnp.inf)
    row_max = jnp.max(scores, axis=1, keepdims=True)
    exp_scores = jnp.exp(scores - row_max)
    row_total = jnp.sum(exp_scores, axis=1, keepdims=True)
    probs = (exp_scores / row_total).astype(jnp.bfloat16)
    return jnp.dot(probs, head_values, preferred_element_type=jnp.float32).astype(jnp.bfloat16)


def local_attention(attn_queries, attn_keys, attn_values):
    batch, length, width = attn_queries.shape
    heads = width // HEAD_DIM

    def split_heads(array):
        return jnp.transpose(array.reshape(batch, length, heads, HEAD_DIM), (0, 2, 1, 3)).reshape(
            batch * heads, length, HEAD_DIM
        )

    outputs = lax.map(
        attend_head, (split_heads(attn_queries), split_heads(attn_keys), split_heads(attn_values))
    )
    return jnp.transpose(outputs.reshape(batch, heads, length, HEAD_DIM), (0, 2, 1, 3)).reshape(
        batch, length, width
    )


def per_device(tokens, expert_ids, router, w_up, w_down, attn_queries, attn_keys, attn_values):
    per_block, local_width = tokens.shape
    experts = router.shape[1]
    block_count = lax.axis_size("dp")
    split_count = block_count // experts
    cap_range = jnp.arange(CAP, dtype=jnp.int32)
    expert_range = jnp.arange(experts, dtype=jnp.int32)
    feature_start = lax.axis_index("section") * local_width
    router_rows = lax.dynamic_slice_in_dim(router, feature_start, local_width, 0)
    partial_logits = jnp.dot(tokens, router_rows, preferred_element_type=jnp.float32)
    logits = lax.psum(partial_logits, "section")
    id_onehot = (expert_ids[:, :, None] == expert_range[None, None, :]).astype(jnp.float32)
    chosen = jnp.sum(logits[:, None, :] * id_onehot, axis=2)
    first_prob = jax.nn.sigmoid(chosen[:, 0] - chosen[:, 1])
    pair_prob = jnp.stack([first_prob, 1.0 - first_prob], axis=1)
    slot_rank = route_slots(expert_ids, 1, per_block, experts)
    matched = (expert_ids[:, :, None] == expert_range)[..., None] & (
        slot_rank[:, :, None, None] == cap_range
    )
    selector = jnp.any(matched, axis=1).astype(jnp.bfloat16)
    packed = jnp.einsum("tec,td->ecd", selector, tokens, preferred_element_type=jnp.float32).astype(
        jnp.bfloat16
    )
    outgoing = jnp.repeat(packed, split_count, axis=0)
    received = lax.all_to_all(outgoing, "dp", split_axis=0, concat_axis=0, tiled=True)
    flat_rows = received.reshape(block_count * CAP, local_width)
    up_weight = w_up[0]
    projected = jnp.dot(
        lax.all_gather(flat_rows, "section", axis=1, tiled=True),
        up_weight,
        preferred_element_type=jnp.float32,
    )
    activated = jax.nn.silu(projected).astype(jnp.bfloat16)
    model_width = w_down.shape[2]
    partial_value = jnp.dot(activated, w_down[0], preferred_element_type=jnp.float32).reshape(
        block_count, CAP, model_width
    )
    summed = lax.psum_scatter(partial_value, "section", scatter_dimension=2, tiled=True)
    returned = lax.all_to_all(summed, "dp", split_axis=0, concat_axis=0, tiled=True)
    attended = local_attention(attn_queries, attn_keys, attn_values)
    group_expert = jnp.arange(block_count, dtype=jnp.int32) // split_count
    on_expert = (expert_ids[:, :, None] == group_expert[None, None, :]).astype(jnp.float32)
    on_slot = (slot_rank[:, :, None] == cap_range[None, None, :]).astype(jnp.float32)
    coefficient = jnp.einsum(
        "tk,tkg,tkc->tgc", pair_prob, on_expert, on_slot, precision=lax.Precision.HIGHEST
    )
    mixed = jnp.einsum("tgc,gcd->td", coefficient, returned, precision=lax.Precision.HIGHEST)
    return (mixed.astype(jnp.bfloat16), attended)


def solution(mesh):
    placed = (
        P("dp", "section"),
        P("dp", None),
        P(),
        P("dp", None, "section"),
        P("dp", "section", None),
        P("dp", None, "section"),
        P("dp", None, "section"),
        P("dp", None, "section"),
    )
    return jax.shard_map(
        per_device,
        mesh=mesh,
        in_specs=placed,
        out_specs=(P("dp", "section"), P("dp", None, "section")),
        check_vma=False,
    )
```

profile of v0, /device:TPU:0, one launch (start us, length us, event | category | flops | bytes accessed | tf_op | source)
XLA Modules:
  0.0 115.8 jit_solution(7374508691938305532)
XLA Ops:
  7.2 0.8 copy.61
  8.0 0.1 eq.88
  8.2 0.2 select_reduce_fusion.1
  8.6 0.1 copy.65
  8.7 0.1 and_reduce_fusion
  8.8 1.0 convolution_convert_fusion.1
  9.8 0.7 copy.67
  10.5 7.3 %all-to-all-start = ((bf16[8,4,1536]{2,1,0:T(4,128)(2,1)}), bf16[8,4,1536]{2,1,0:T(4,128)(2,1)S(1)}, u32[]{:S(2)}, u32[]{:S(2)}) async-start(bf16[8,4,1536]{2,1,0:T(4,128)(2,1)} %copy.67), calls=%async_computation | async-start | bytes 196608 | tf_op jit(solution)/shard_map/all_to_all | solution.py:79
  17.8 1.2 %copy.71 = bf16[1,128,1536]{1,2,0:T(8,128)(2,1)S(1)} copy(bf16[1,128,1536]{2,1,0:T(8,128)(2,1)} %param.15) | data formatting | bytes 786432 | tf_op args[5]
  19.0 1.2 %copy.72 = bf16[1,128,1536]{1,2,0:T(8,128)(2,1)S(1)} copy(bf16[1,128,1536]{2,1,0:T(8,128)(2,1)} %param.16) | data formatting | bytes 786432 | tf_op args[6]
  20.2 1.2 %copy.73 = bf16[1,128,1536]{1,2,0:T(8,128)(2,1)S(1)} copy(bf16[1,128,1536]{2,1,0:T(8,128)(2,1)} %param.17) | data formatting | bytes 786432 | tf_op args[7]
  21.5 3.4 %all-to-all-done = bf16[8,4,1536]{2,1,0:T(4,128)(2,1)S(1)} async-done(((bf16[8,4,1536]{2,1,0:T(4,128)(2,1)}), bf16[8,4,1536]{2,1,0:T(4,128)(2,1)S(1)}, u32[]{:S(2)}, u32[]{:S(2)}) %all-to-all-start) | async-done | bytes 98336 | tf_op jit(solution)/shard_map/all_to_all | solution.py:79
  24.9 6.5 %all_gather.3 = bf16[32,6144]{1,0:T(8,128)(2,1)S(1)} all-gather(bf16[32,1536]{1,0:T(8,128)(2,1)S(1)} %reshape.136), channel_id=1, replica_groups=mesh['section'=4,'dp'=8] {'section'}, dimensions={1}, use_global_device_ids=true | all-gather | bytes 491520 | tf_op jit(solution)/shard_map/all_gather | solution.py:83
  31.4 19.9 %multiply_convert_fusion = bf16[32,4096]{1,0:T(8,128)(2,1)S(1)} fusion(bf16[32,6144]{1,0:T(8,128)(2,1)S(1)} %all_gather.3, bf16[1,6144,4096]{2,1,0:T(8,128)(2,1)} %param.13), kind=kOutput, calls=%fused_computation.27 | convolution fusion | flops 1611268096 | bytes 50987008 | tf_op jit(solution)/shard_map/dot_general | solution.py:82
  51.3 0.1 dot_general.40
  51.4 20.4 %fusion.13 = f32[8,4,6144]{2,0,1:T(8,128)} fusion(bf16[1,4096,6144]{2,1,0:T(8,128)(2,1)} %param.14, bf16[8,4,4096]{2,1,0:T(4,128)(2,1)S(1)} %dot_general.40), kind=kOutput, calls=%fused_computation.19 | convolution fusion | flops 1610612736 | bytes 51380224 | tf_op jit(solution)/shard_map/dot_general | solution.py:89
  71.8 7.6 %while.10 = (s32[]{:T(128)}, bf16[12,128,128]{1,2,0:T(8,128)(2,1)S(1)}, bf16[12,128,128]{1,2,0:T(8,128)(2,1)S(1)}, bf16[12,128,128]{1,2,0:T(8,128)(2,1)S(1)}, bf16[12,128,128]{1,2,0:T(8,128)(2,1)S(1)}, /*index=5*/s32[]{:T(128)}) while((s32[]{:T(128)}, bf16[12,128,128]{1,2,0:T(8,128)(2,1)S(1)}, bf16[12,128,128]{1,2,0:T(8,128)(2,1)S(1)}, ...), condition=%wide.region_9.10_spmd, body=%wide.region_6.9_spmd.sunk | while | flops 8552194 | bytes 462413 | solution.py:47
  71.8 0.2 fusion.41
  72.1 0.2 fusion.43
  72.3 0.1 copy.88
  72.5 0.2 fusion.41
  72.7 0.2 fusion.43
  72.9 0.1 copy.88
  73.1 0.2 fusion.41
  73.4 0.2 fusion.43
  73.6 0.1 copy.88
  73.7 0.2 fusion.41
  74.0 0.2 fusion.43
  74.2 0.1 copy.88
  74.4 0.2 fusion.41
  74.6 0.2 fusion.43
  74.8 0.1 copy.88
  75.0 0.2 fusion.41
  75.3 0.2 fusion.43
  75.5 0.1 copy.88
  75.6 0.2 fusion.41
  75.9 0.2 fusion.43
  76.1 0.1 copy.88
  76.3 0.2 fusion.41
  76.5 0.2 fusion.43
  76.7 0.1 copy.88
  76.9 0.2 fusion.41
  77.2 0.2 fusion.43
  77.4 0.1 copy.88
  77.5 0.2 fusion.41
  77.8 0.2 fusion.43
  78.0 0.1 copy.88
  78.2 0.2 fusion.41
  78.4 0.2 fusion.43
  78.6 0.1 copy.88
  78.8 0.2 fusion.41
  79.1 0.2 fusion.43
  79.3 0.1 copy.88
  79.4 0.1 convolution_bitcast_fusion.1
  79.6 6.8 %psum.7 = f32[8,8]{0,1:T(8,128)S(1)} all-reduce(f32[8,8]{0,1:T(8,128)S(1)} %convolution_bitcast_fusion.1), channel_id=1, replica_groups=mesh['section'=4,'dp'=8] {'section'}, use_global_device_ids=true, to_apply=%region_2.0 | all-reduce | flops 64 | bytes 512 | tf_op jit(solution)/shard_map/psum | solution.py:65
  86.4 0.2 select_reduce_fusion
  86.6 6.4 %reduce-scatter.2.cloned.1.call-done = f32[8,4,1536]{2,0,1:T(8,128)} async-done(((f32[8,4,6144]{2,0,1:T(8,128)}), f32[8,4,1536]{2,0,1:T(8,128)}) %reduce-scatter.2.cloned.1.call-update) | async-done | bytes 196624 | tf_op jit(solution)/shard_map/reduce_scatter | solution.py:92
  93.0 1.7 %copy.69 = f32[8,4,1536]{2,1,0:T(4,128)} copy(f32[8,4,1536]{2,0,1:T(8,128)} %reduce-scatter.2.cloned.1.call-done) | data formatting | bytes 393216 | tf_op jit(solution)/shard_map/reduce_scatter | solution.py:92
  94.7 5.5 %all-to-all-start.1 = ((f32[8,4,1536]{2,1,0:T(4,128)}), f32[8,4,1536]{2,1,0:T(4,128)S(1)}, u32[]{:S(2)}, u32[]{:S(2)}) async-start(f32[8,4,1536]{2,1,0:T(4,128)} %copy.69), calls=%async_computation.2 | async-start | bytes 393216 | tf_op jit(solution)/shard_map/all_to_all | solution.py:93
  100.3 0.3 fusion.23
  100.7 0.1 copy.70
  100.8 0.9 copy.78
  101.7 6.3 %all-to-all-done.1 = f32[8,4,1536]{2,1,0:T(4,128)S(1)} async-done(((f32[8,4,1536]{2,1,0:T(4,128)}), f32[8,4,1536]{2,1,0:T(4,128)S(1)}, u32[]{:S(2)}, u32[]{:S(2)}) %all-to-all-start.1) | async-done | bytes 196640 | tf_op jit(solution)/shard_map/all_to_all | solution.py:93
  108.0 0.9 fusion.17
  (41 shorter events, 1.4 us)
Async XLA Ops:
  7.2 72.3 %copy-start = (bf16[6144,8]{0,1:T(8,128)(2,1)S(1)}, bf16[6144,8]{0,1:T(8,128)(2,1)}, u32[]{:S(2)}) copy-start(bf16[6144,8]{0,1:T(8,128)(2,1)} %param.12) | copy-start | bytes 294916
  10.5 14.4 %all-to-all-start = ((bf16[8,4,1536]{2,1,0:T(4,128)(2,1)}), bf16[8,4,1536]{2,1,0:T(4,128)(2,1)S(1)}, u32[]{:S(2)}, u32[]{:S(2)}) async-start(bf16[8,4,1536]{2,1,0:T(4,128)(2,1)} %copy.67), calls=%async_computation | async-start | bytes 196608 | tf_op jit(solution)/shard_map/all_to_all | solution.py:79
  17.7 75.2 %reduce-scatter.2.cloned.1.call-start = ((), (), s32[]{:S(2)}) async-start(), calls=%async_computation.3 | async-start | bytes 983040 | tf_op jit(solution)/shard_map/reduce_scatter | solution.py:92
  31.4 48.1 %copy-start.1 = (bf16[8,1536]{1,0:T(8,128)(2,1)S(1)}, bf16[8,1536]{1,0:T(8,128)(2,1)}, u32[]{:S(2)}) copy-start(bf16[8,1536]{1,0:T(8,128)(2,1)} %param.10) | copy-start | bytes 73732
  94.7 13.3 %all-to-all-start.1 = ((f32[8,4,1536]{2,1,0:T(4,128)}), f32[8,4,1536]{2,1,0:T(4,128)S(1)}, u32[]{:S(2)}, u32[]{:S(2)}) async-start(f32[8,4,1536]{2,1,0:T(4,128)} %copy.69), calls=%async_computation.2 | async-start | bytes 393216 | tf_op jit(solution)/shard_map/all_to_all | solution.py:93
Sparse Core Ops, SparseCore 0:
  71.9 20.9 reduce-scatter.1
where the time goes:
time: 116 us
  matrix products  47.8 us (41%)
  waiting for transfers between devices  16.1 us (14%)
  between operations  14.1 us (12%)
  blocking collectives  13.2 us (11%)
  starting transfers between devices  12.8 us (11%)
  local copies, waits for them, and re-layouts  9.87 us (9%)
  other arithmetic  1.37 us (1%)
    dot_general x1, matrix products, per_device(): jnp.dot(activated, w_down[0], preferred_element_type=jnp.float32)  20.4 us
    dot_general x1, matrix products, per_device(): jnp.dot(lax.all_gather(flat_rows, 'section', axis=1, tiled=True), up_weig...  19.9 us
    all_to_all x1, starting transfers between devices, per_device(): lax.all_to_all(outgoing, 'dp', split_axis=0, concat_axis=0, tiled=True)  7.28 us
    psum x1, blocking collectives, per_device(): logits = lax.psum(partial_logits, 'section')  6.75 us
    all_gather x1, blocking collectives, per_device(): lax.all_gather(flat_rows, 'section', axis=1, tiled=True)  6.49 us
    reduce_scatter x1, waiting for transfers between devices, per_device(): lax.psum_scatter(partial_value, 'section', scatter_dimension=2, tiled=True)  6.41 us
    all_to_all x1, waiting for transfers between devices, per_device(): lax.all_to_all(summed, 'dp', split_axis=0, concat_axis=0, tiled=True)  6.28 us
    all_to_all x1, starting transfers between devices, per_device(): lax.all_to_all(summed, 'dp', split_axis=0, concat_axis=0, tiled=True)  5.5 us
  transfers between devices with their start and end apart: 3, of which 3 were waited for; matrix products, arithmetic and copies ran while one was open for 11% of the time, Pallas kernels for 0%

commit v1 on v0

v1 whole, which is shorter than its diff:
```python
import functools
import math

import jax
import jax.numpy as jnp
from jax import lax
from jax.experimental import pallas as pl
from jax.experimental.pallas import tpu as pltpu
from jax.sharding import PartitionSpec as P

HEAD_DIM = 128
MESH = pl.DeviceIdType.MESH


def aligned(index, size):
    return pl.ds(pl.multiple_of(index * size, size), size)


def kernel(
    dims,
    tokens_hbm,
    ids_hbm,
    router_hbm,
    up_hbm,
    down_hbm,
    q_hbm,
    k_hbm,
    v_hbm,
    mixed_hbm,
    attended_hbm,
    ring,
    x_all,
    x_rows,
    hidden,
    stage,
    received,
    router,
    ids,
    logits,
    q,
    k,
    v,
    attended,
    mixed,
    small_sem,
    up_sem,
    down_sem,
    send_sem,
    x_sem,
    back_sem,
    part_sem,
    own_sem,
    out_sem,
):
    n_sec, n_dp, rows, cols, experts = dims
    per_block, width = tokens_hbm.shape
    model, ff = up_hbm.shape[1:]
    devices = n_sec * n_dp
    up_blocks, up_units = ff // cols, model // rows
    down_blocks, down_units = model // cols, ff // rows
    sec_blocks = width // cols
    s, g = lax.axis_index("section"), lax.axis_index("dp")
    me = s * n_dp + g

    copies = [
        pltpu.make_async_copy(tokens_hbm, x_all.at[me], small_sem.at[0]),
        pltpu.make_async_copy(q_hbm.at[0], q, small_sem.at[1]),
        pltpu.make_async_copy(k_hbm.at[0], k, small_sem.at[2]),
        pltpu.make_async_copy(v_hbm.at[0], v, small_sem.at[3]),
        pltpu.make_async_copy(router_hbm, router, small_sem.at[4]),
        pltpu.make_async_copy(ids_hbm, ids, small_sem.at[5]),
    ]
    for copy in copies:
        copy.start()

    def up_copy(n):
        return pltpu.make_async_copy(
            up_hbm.at[0, :, aligned(n, cols)], ring.at[aligned(n, model)], up_sem.at[n]
        )

    @pl.loop(0, up_blocks)
    def _(n):
        up_copy(n).start()

    barrier = pltpu.get_barrier_semaphore()

    def place(index):
        return {"section": index // n_dp, "dp": index % n_dp}

    @pl.loop(1, devices)
    def _(offset):
        peer = (me + offset) % devices
        pl.semaphore_signal(barrier, inc=1, device_id=place(peer), device_id_type=MESH)

    copies[0].wait()
    pl.semaphore_wait(barrier, devices - 1)

    @pl.loop(1, devices)
    def _(offset):
        peer = (me + offset) % devices
        pltpu.make_async_remote_copy(
            src_ref=x_all.at[me],
            dst_ref=x_all.at[me],
            send_sem=send_sem,
            recv_sem=x_sem,
            device_id=place(peer),
            device_id_type=MESH,
        ).start()

    for copy in copies[1:4]:
        copy.wait()
    length = q.shape[0]
    heads = width // HEAD_DIM
    group = math.gcd(heads, 4)
    causal = lax.broadcasted_iota(jnp.int32, (length, length), 1) <= lax.broadcasted_iota(
        jnp.int32, (length, length), 0
    )

    @pl.loop(0, heads // group)
    def _(step):
        for lane in range(group):
            at = aligned(step * group + lane, HEAD_DIM)
            scores = lax.dot_general(
                q[:, at], k[:, at], (((1,), (1,)), ((), ())), preferred_element_type=jnp.float32
            ) * (1.0 / math.sqrt(HEAD_DIM))
            scores = jnp.where(causal, scores, -jnp.inf)
            exps = jnp.exp(scores - jnp.max(scores, axis=1, keepdims=True))
            probs = (exps / jnp.sum(exps, axis=1, keepdims=True)).astype(jnp.bfloat16)
            attended[:, at] = jnp.dot(
                probs, v[:, at], preferred_element_type=jnp.float32
            ).astype(jnp.bfloat16)

    attended_copy = pltpu.make_async_copy(attended, attended_hbm.at[0], out_sem.at[0])
    attended_copy.start()

    others = x_all.at[pl.ds(0, devices - 1)]
    pltpu.make_async_copy(others, others, x_sem).wait()
    for part in range(n_sec):
        at = pl.ds(part * width, width)
        for pair in range(n_dp // 2):
            first = x_all[part * n_dp + 2 * pair].astype(jnp.float32)
            second = x_all[part * n_dp + 2 * pair + 1].astype(jnp.float32)
            x_rows[pl.ds(2 * pair * per_block, 2 * per_block), at] = jnp.concatenate(
                [first, second], axis=0
            ).astype(jnp.bfloat16)

    def down_place(block):
        return (s + 1 + block // sec_blocks) % n_sec, block % sec_blocks

    def down_copy(unit):
        block, part = unit // down_units, unit % down_units
        sec, col = down_place(block)
        return pltpu.make_async_copy(
            down_hbm.at[0, aligned(part, rows), aligned(sec * sec_blocks + col, cols)],
            ring.at[aligned(unit, rows)],
            down_sem.at[block],
        )

    @pl.loop(0, up_blocks)
    def _(n):
        up_copy(n).wait()
        value = jnp.dot(
            x_rows[...], ring[aligned(n, model), :], preferred_element_type=jnp.float32
        )
        hidden[:, aligned(n, cols)] = (value / (1.0 + jnp.exp(-value))).astype(jnp.bfloat16)
        for unit in range(up_units):
            down_copy(n * up_units + unit).start()

    copies[4].wait()
    copies[5].wait()
    logits[...] = lax.dot_general(
        x_rows[...], router[...], (((1,), (1,)), ((), ())), preferred_element_type=jnp.float32
    )
    own = logits[aligned(g, per_block), :]
    lanes = lax.broadcasted_iota(jnp.int32, (per_block, experts), 1)
    diagonal = lax.broadcasted_iota(jnp.int32, (per_block, per_block), 0) == lax.broadcasted_iota(
        jnp.int32, (per_block, per_block), 1
    )

    def column(which):
        row = jnp.broadcast_to(ids[which : which + 1, :].astype(jnp.float32), diagonal.shape)
        return jnp.sum(jnp.where(diagonal, row, 0.0), axis=1, keepdims=True).astype(jnp.int32)

    is_first, is_second = column(0) == lanes, column(1) == lanes
    gap = jnp.sum(jnp.where(is_first, own, 0.0), axis=1, keepdims=True) - jnp.sum(
        jnp.where(is_second, own, 0.0), axis=1, keepdims=True
    )
    first_prob = 1.0 / (1.0 + jnp.exp(-gap))
    coefficient = jnp.where(is_first, first_prob, 0.0) + jnp.where(
        is_second, 1.0 - first_prob, 0.0
    )

    def down_block(block):
        taken = ring.at[aligned(block, ff)]
        pltpu.make_async_copy(taken, taken, down_sem.at[block]).wait()
        partial = jnp.dot(hidden[...], taken[...], preferred_element_type=jnp.float32)
        for b in range(n_dp):
            stage[block, b] = partial[b * per_block : (b + 1) * per_block].astype(jnp.bfloat16)

    def send_back(block, first):
        sec, col = down_place(block)

        @pl.loop(first, n_dp)
        def _(offset):
            b = (g + offset) % n_dp
            pltpu.make_async_remote_copy(
                src_ref=stage.at[block, b],
                dst_ref=received.at[me, :, aligned(col, cols)],
                send_sem=part_sem,
                recv_sem=back_sem,
                device_id={"section": sec, "dp": b},
                device_id_type=MESH,
            ).start()

    away = (n_sec - 1) * sec_blocks

    @pl.loop(0, away)
    def _(block):
        down_block(block)
        send_back(block, 0)

    @pl.loop(away, down_blocks)
    def _(block):
        down_block(block)
        send_back(block, 1)
        pltpu.make_async_copy(
            stage.at[block, g],
            received.at[me, :, aligned(block - away, cols)],
            own_sem,
        ).start()

    own_row = received.at[me]
    pltpu.make_async_copy(own_row, own_row, own_sem).wait()
    rest = received.at[pl.ds(0, devices - 1)]
    pltpu.make_async_copy(rest, rest, back_sem).wait()

    shares = [
        jnp.broadcast_to(coefficient[:, e : e + 1], (per_block, width)) for e in range(experts)
    ]
    per_expert = n_dp // experts

    def add(part, total):
        for b in range(n_dp):
            total += shares[b // per_expert] * received[part * n_dp + b].astype(jnp.float32)
        return total

    total = lax.fori_loop(0, n_sec, add, jnp.zeros((per_block, width), jnp.float32))
    mixed[...] = total.astype(jnp.bfloat16)
    mixed_copy = pltpu.make_async_copy(mixed, mixed_hbm, out_sem.at[1])
    mixed_copy.start()

    pltpu.make_async_copy(others, others, send_sem).wait()
    pltpu.make_async_copy(rest, rest, part_sem).wait()
    attended_copy.wait()
    mixed_copy.wait()


def per_device(tokens, expert_ids, router, w_up, w_down, attn_queries, attn_keys, attn_values):
    n_sec, n_dp = lax.axis_size("section"), lax.axis_size("dp")
    per_block, width = tokens.shape
    model, experts = router.shape
    ff = w_up.shape[2]
    length = attn_queries.shape[1]
    devices = n_sec * n_dp
    rows, cols = math.gcd(model, ff), math.gcd(ff, width)
    down_blocks = model // cols
    bf16, f32 = jnp.bfloat16, jnp.float32
    any_spec = pl.BlockSpec(memory_space=pl.ANY)
    return pl.pallas_call(
        functools.partial(kernel, (n_sec, n_dp, rows, cols, experts)),
        out_shape=(
            jax.ShapeDtypeStruct(tokens.shape, bf16),
            jax.ShapeDtypeStruct(attn_queries.shape, bf16),
        ),
        in_specs=[any_spec] * 8,
        out_specs=(any_spec, any_spec),
        scratch_shapes=[
            pltpu.VMEM((model * ff // cols, cols), bf16),
            pltpu.VMEM((devices, per_block, width), bf16),
            pltpu.VMEM((n_dp * per_block, model), bf16),
            pltpu.VMEM((n_dp * per_block, ff), bf16),
            pltpu.VMEM((down_blocks, n_dp, per_block, cols), bf16),
            pltpu.VMEM((devices, per_block, width), bf16),
            pltpu.VMEM((experts, model), bf16),
            pltpu.VMEM((2, per_block), jnp.int32),
            pltpu.VMEM((n_dp * per_block, experts), f32),
            pltpu.VMEM((length, width), bf16),
            pltpu.VMEM((length, width), bf16),
            pltpu.VMEM((length, width), bf16),
            pltpu.VMEM((length, width), bf16),
            pltpu.VMEM((per_block, width), bf16),
            pltpu.SemaphoreType.DMA((6,)),
            pltpu.SemaphoreType.DMA((ff // cols,)),
            pltpu.SemaphoreType.DMA((down_blocks,)),
            pltpu.SemaphoreType.DMA,
            pltpu.SemaphoreType.DMA,
            pltpu.SemaphoreType.DMA,
            pltpu.SemaphoreType.DMA,
            pltpu.SemaphoreType.DMA,
            pltpu.SemaphoreType.DMA((2,)),
        ],
        compiler_params=pltpu.CompilerParams(
            collective_id=0, has_side_effects=True, vmem_limit_bytes=67043328
        ),
    )(tokens, expert_ids.T, router.T, w_up, w_down, attn_queries, attn_keys, attn_values)


def solution(mesh):
    placed = (
        P("dp", "section"),
        P("dp", None),
        P(),
        P("dp", None, "section"),
        P("dp", "section", None),
        P("dp", None, "section"),
        P("dp", None, "section"),
        P("dp", None, "section"),
    )
    return jax.shard_map(
        per_device,
        mesh=mesh,
        in_specs=placed,
        out_specs=(P("dp", "section"), P("dp", None, "section")),
        check_vma=False,
    )
```

time: 116 us -> 61.3 us (0.53)
  Pallas kernels: 0 us -> 57.3 us
  matrix products: 47.8 us -> 0 us
  waiting for transfers between devices: 16.1 us -> 0 us
  between operations: 14.1 us -> 0.64 us
  blocking collectives: 13.2 us -> 0 us
  starting transfers between devices: 12.8 us -> 0 us
  local copies, waits for them, and re-layouts: 9.87 us -> 3.11 us
  other arithmetic: 1.37 us -> 0 us
    pallas_call x0 -> x1, Pallas kernels: none -> 57.3 us  [per_device(): pl.pallas_call(functools.partial(kernel, (n_sec, n_dp, rows, cols, expert...]
    dot_general x30 -> x0, matrix products: 47.8 us -> none  [the longest x1 20.4 us: per_device(): jnp.dot(activated, w_down[0], preferred_element_type=jnp.float32)]
    all_to_all x2 -> x0, starting transfers between devices: 12.8 us -> none  [the longest x1 7.28 us: per_device(): lax.all_to_all(outgoing, 'dp', split_axis=0, concat_axis=0, tiled=True)]
    all_to_all x2 -> x0, waiting for transfers between devices: 9.68 us -> none  [the longest x1 6.28 us: per_device(): lax.all_to_all(summed, 'dp', split_axis=0, concat_axis=0, tiled=True)]
    psum x1 -> x0, blocking collectives: 6.75 us -> none  [per_device(): logits = lax.psum(partial_logits, 'section')]
    all_gather x1 -> x0, blocking collectives: 6.49 us -> none  [per_device(): lax.all_gather(flat_rows, 'section', axis=1, tiled=True)]
    reduce_scatter x1 -> x0, waiting for transfers between devices: 6.41 us -> none  [per_device(): lax.psum_scatter(partial_value, 'section', scatter_dimension=2, tiled=True)]
    unnamed x9 -> x2, local copies, waits for them, and re-layouts: 5.38 us -> 3.11 us
  transfers between devices with their start and end apart: 3 -> 0, of which waited for: 3 -> 0; matrix products, arithmetic and copies ran while one was open for 11% -> 0% of each run, Pallas kernels for 0% -> 0%
where the time goes in v1:
time: 61.3 us; the launch traced here: 61 us
  Pallas kernels  57.3 us (93%)
  local copies, waits for them, and re-layouts  3.11 us (5%)
  between operations  0.64 us (1%)
    pallas_call x1, Pallas kernels, per_device(): pl.pallas_call(functools.partial(kernel, (n_sec, n_dp, rows, cols, expert...  57.3 us
    unnamed x2, local copies, waits for them, and re-layouts  3.11 us

profile of v1, /device:TPU:0, one launch (start us, length us, event | category | flops | bytes accessed | tf_op | source)
XLA Modules:
  0.0 61.0 jit_solution(14604690739410318202)
XLA Ops:
  0.6 57.3 %shard_map.95 = (bf16[8,1536]{1,0:T(8,128)(2,1)}, bf16[1,128,1536]{2,1,0:T(8,128)(2,1)}) custom-call(bf16[8,1536]{1,0:T(8,128)(2,1)} %tokens_hbm.1, s32[2,8]{1,0:T(2,128)} %bitcast.3, bf16[8,6144]{1,0:T(8,128)(2,1)} %bitcast.2, bf16[1,6144,4096]{2,1,0:T(8,128)(2,1)} %up_hbm.1, bf16[1,4096,6144]{2,1,0:T(8,128)(2,1)} %down_hbm.1, bf16[1,128,1536]{2,1,0:T(8,128)(2,1)} %q_hbm.1, ...), custom_call_target="tpu_custom_call" | custom-call | tf_op jit(solution)/shard_map/pallas_call | solution.py:269
  57.9 1.3 %copy.12 = bf16[8,1536]{1,0:T(8,128)(2,1)} copy(bf16[8,1536]{1,0:T(8,128)(2,1)} %get-tuple-element.4) | data formatting | bytes 49152
  59.3 1.8 %copy.13 = bf16[1,128,1536]{2,1,0:T(8,128)(2,1)} copy(bf16[1,128,1536]{2,1,0:T(8,128)(2,1)} %get-tuple-element.5) | data formatting | bytes 786432

commit v2 on v1

--- a/solution.py
+++ b/solution.py
@@ -33,6 +33,8 @@
     x_rows,
     hidden,
     stage,
+    terms,
+    returning,
     received,
     router,
     ids,
@@ -46,7 +48,10 @@
     up_sem,
     down_sem,
     send_sem,
+    line_sem,
+    plane_sem,
     x_sem,
+    term_sem,
     back_sem,
     part_sem,
     own_sem,
@@ -61,9 +66,16 @@
     sec_blocks = width // cols
     s, g = lax.axis_index("section"), lax.axis_index("dp")
     me = s * n_dp + g
+    half, lines = n_sec // 2, n_dp // 2
+    y, core, line, x = s // 2, s % 2, g // 2, g % 2
+
+    def slot(y_at, core_at, dp):
+        return (core_at * half + y_at) * n_dp + dp
+
+    mine = slot(y, core, g)
 
     copies = [
-        pltpu.make_async_copy(tokens_hbm, x_all.at[me], small_sem.at[0]),
+        pltpu.make_async_copy(tokens_hbm, x_all.at[mine], small_sem.at[0]),
         pltpu.make_async_copy(q_hbm.at[0], q, small_sem.at[1]),
         pltpu.make_async_copy(k_hbm.at[0], k, small_sem.at[2]),
         pltpu.make_async_copy(v_hbm.at[0], v, small_sem.at[3]),
@@ -92,21 +104,6 @@
         peer = (me + offset) % devices
         pl.semaphore_signal(barrier, inc=1, device_id=place(peer), device_id_type=MESH)
 
-    copies[0].wait()
-    pl.semaphore_wait(barrier, devices - 1)
-
-    @pl.loop(1, devices)
-    def _(offset):
-        peer = (me + offset) % devices
-        pltpu.make_async_remote_copy(
-            src_ref=x_all.at[me],
-            dst_ref=x_all.at[me],
-            send_sem=send_sem,
-            recv_sem=x_sem,
-            device_id=place(peer),
-            device_id_type=MESH,
-        ).start()
-
     for copy in copies[1:4]:
         copy.wait()
     length = q.shape[0]
@@ -116,8 +113,11 @@
         jnp.int32, (length, length), 0
     )
 
-    @pl.loop(0, heads // group)
-    def _(step):
+    def attend(third):
+        steps = heads // group
+        pl.loop(steps * third // 3, steps * (third + 1) // 3)(attend_heads)
+
+    def attend_heads(step):
         for lane in range(group):
             at = aligned(step * group + lane, HEAD_DIM)
             scores = lax.dot_general(
@@ -130,13 +130,59 @@
                 probs, v[:, at], preferred_element_type=jnp.float32
             ).astype(jnp.bfloat16)
 
+    attend(0)
+    copies[0].wait()
+    pl.semaphore_wait(barrier, devices - 1)
+
+    def send_tokens(block, sem, place):
+        pltpu.make_async_remote_copy(
+            src_ref=x_all.at[block],
+            dst_ref=x_all.at[block],
+            send_sem=send_sem,
+            recv_sem=sem,
+            device_id=place,
+            device_id_type=MESH,
+        ).start()
+
+    @pl.loop(1, lines)
+    def _(offset):
+        to = (line + offset) % lines
+        send_tokens(mine, line_sem.at[offset], {"section": s, "dp": to * 2 + x})
+
+    def spread(from_line):
+        block = slot(y, core, from_line * 2 + x)
+
+        @pl.loop(1, 2 * half)
+        def _(offset):
+            to_y, to_x = (y + offset // 2) % half, (x + offset) % 2
+            send_tokens(
+                block, plane_sem, {"section": to_y * 2 + core, "dp": line * 2 + to_x}
+            )
+
+    spread(line)
+    attend(1)
+
+    @pl.loop(1, lines)
+    def _(offset):
+        from_line = (line + lines - offset) % lines
+        block = x_all.at[slot(y, core, from_line * 2 + x)]
+        pltpu.make_async_copy(block, block, line_sem.at[offset]).wait()
+        spread(from_line)
+
+    n_half = half * n_dp
+    plane = x_all.at[pl.ds(0, n_half - lines)]
+    pltpu.make_async_copy(plane, plane, plane_sem).wait()
+    send_tokens(pl.ds(core * n_half, n_half), x_sem, {"section": y * 2 + 1 - core, "dp": g})
+
+    attend(2)
     attended_copy = pltpu.make_async_copy(attended, attended_hbm.at[0], out_sem.at[0])
     attended_copy.start()
 
     others = x_all.at[pl.ds(0, devices - 1)]
-    pltpu.make_async_copy(others, others, x_sem).wait()
+    arrived = x_all.at[pl.ds(0, n_half)]
+    pltpu.make_async_copy(arrived, arrived, x_sem).wait()
     for part in range(n_sec):
-        at = pl.ds(part * width, width)
+        at = pl.ds((part % half * 2 + part // half) * width, width)
         for pair in range(n_dp // 2):
             first = x_all[part * n_dp + 2 * pair].astype(jnp.float32)
             second = x_all[part * n_dp + 2 * pair + 1].astype(jnp.float32)
@@ -145,7 +191,9 @@
             ).astype(jnp.bfloat16)
 
     def down_place(block):
-        return (s + 1 + block // sec_blocks) % n_sec, block % sec_blocks
+        turn = block // sec_blocks
+        to_y, to_core = (y + 1 + turn // 2) % half, (core + 1 + turn) % 2
+        return to_y * 2 + to_core, block % sec_blocks
 
     def down_copy(unit):
         block, part = unit // down_units, unit % down_units
@@ -193,45 +241,55 @@
     def down_block(block):
         taken = ring.at[aligned(block, ff)]
         pltpu.make_async_copy(taken, taken, down_sem.at[block]).wait()
-        partial = jnp.dot(hidden[...], taken[...], preferred_element_type=jnp.float32)
+        return jnp.dot(hidden[...], taken[...], preferred_element_type=jnp.float32)
+
+    away = (n_sec - 1) * sec_blocks
+
+    @pl.loop(0, away)
+    def _(block):
+        stage[block] = down_block(block).astype(jnp.bfloat16)
+        sec, col = down_place(block)
+        pltpu.make_async_remote_copy(
+            src_ref=stage.at[block],
+            dst_ref=terms.at[block // sec_blocks, :, aligned(col, cols)],
+            send_sem=term_sem.at[0],
+            recv_sem=term_sem.at[1],
+            device_id={"section": sec, "dp": g},
+            device_id_type=MESH,
+        ).start()
+
+    pltpu.make_async_copy(terms, terms, term_sem.at[1]).wait()
+
+    @pl.loop(away, down_blocks)
+    def _(block):
+        at = aligned(block - away, cols)
+        summed = down_block(block)
+        for term in range(n_sec - 1):
+            summed += terms[term, :, at].astype(jnp.float32)
         for b in range(n_dp):
-            stage[block, b] = partial[b * per_block : (b + 1) * per_block].astype(jnp.bfloat16)
-
-    def send_back(block, first):
-        sec, col = down_place(block)
-
-        @pl.loop(first, n_dp)
+            returning[block - away, b] = summed[b * per_block : (b + 1) * per_block].astype(
+                jnp.bfloat16
+            )
+
+        @pl.loop(1, n_dp)
         def _(offset):
             b = (g + offset) % n_dp
             pltpu.make_async_remote_copy(
-                src_ref=stage.at[block, b],
-                dst_ref=received.at[me, :, aligned(col, cols)],
+                src_ref=returning.at[block - away, b],
+                dst_ref=received.at[g, :, at],
                 send_sem=part_sem,
                 recv_sem=back_sem,
-                device_id={"section": sec, "dp": b},
+                device_id={"section": s, "dp": b},
                 device_id_type=MESH,
             ).start()
 
-    away = (n_sec - 1) * sec_blocks
-
-    @pl.loop(0, away)
-    def _(block):
-        down_block(block)
-        send_back(block, 0)
-
-    @pl.loop(away, down_blocks)
-    def _(block):
-        down_block(block)
-        send_back(block, 1)
         pltpu.make_async_copy(
-            stage.at[block, g],
-            received.at[me, :, aligned(block - away, cols)],
-            own_sem,
+            returning.at[block - away, g], received.at[g, :, at], own_sem
         ).start()
 
-    own_row = received.at[me]
+    own_row = received.at[g]
     pltpu.make_async_copy(own_row, own_row, own_sem).wait()
-    rest = received.at[pl.ds(0, devices - 1)]
+    rest = received.at[pl.ds(0, n_dp - 1)]
     pltpu.make_async_copy(rest, rest, back_sem).wait()
 
     shares = [
@@ -239,18 +297,16 @@
     ]
     per_expert = n_dp // experts
 
-    def add(part, total):
-        for b in range(n_dp):
-            total += shares[b // per_expert] * received[part * n_dp + b].astype(jnp.float32)
-        return total
-
-    total = lax.fori_loop(0, n_sec, add, jnp.zeros((per_block, width), jnp.float32))
+    total = jnp.zeros((per_block, width), jnp.float32)
+    for b in range(n_dp):
+        total += shares[b // per_expert] * received[b].astype(jnp.float32)
     mixed[...] = total.astype(jnp.bfloat16)
     mixed_copy = pltpu.make_async_copy(mixed, mixed_hbm, out_sem.at[1])
     mixed_copy.start()
 
     pltpu.make_async_copy(others, others, send_sem).wait()
     pltpu.make_async_copy(rest, rest, part_sem).wait()
+    pltpu.make_async_copy(terms, terms, term_sem.at[0]).wait()
     attended_copy.wait()
     mixed_copy.wait()
 
@@ -279,8 +335,10 @@
             pltpu.VMEM((devices, per_block, width), bf16),
             pltpu.VMEM((n_dp * per_block, model), bf16),
             pltpu.VMEM((n_dp * per_block, ff), bf16),
-            pltpu.VMEM((down_blocks, n_dp, per_block, cols), bf16),
-            pltpu.VMEM((devices, per_block, width), bf16),
+            pltpu.VMEM((down_blocks - width // cols, n_dp * per_block, cols), bf16),
+            pltpu.VMEM((n_sec - 1, n_dp * per_block, width), bf16),
+            pltpu.VMEM((width // cols, n_dp, per_block, cols), bf16),
+            pltpu.VMEM((n_dp, per_block, width), bf16),
             pltpu.VMEM((experts, model), bf16),
             pltpu.VMEM((2, per_block), jnp.int32),
             pltpu.VMEM((n_dp * per_block, experts), f32),
@@ -293,7 +351,10 @@
             pltpu.SemaphoreType.DMA((ff // cols,)),
             pltpu.SemaphoreType.DMA((down_blocks,)),
             pltpu.SemaphoreType.DMA,
-            pltpu.SemaphoreType.DMA,
+            pltpu.SemaphoreType.DMA((n_dp // 2,)),
+            pltpu.SemaphoreType.DMA,
+            pltpu.SemaphoreType.DMA,
+            pltpu.SemaphoreType.DMA((2,)),
             pltpu.SemaphoreType.DMA,
             pltpu.SemaphoreType.DMA,
             pltpu.SemaphoreType.DMA,

time: 61.3 us -> 51.1 us (0.83)
  Pallas kernels: 57.3 us -> 47.1 us
    pallas_call x1, Pallas kernels: 57.3 us -> 47.1 us  [per_device(): pl.pallas_call(functools.partial(kernel, (n_sec, n_dp, rows, cols, expert...]
where the time goes in v2:
time: 51.1 us; the launch traced here: 50.9 us
  Pallas kernels  47.1 us (92%)
  local copies, waits for them, and re-layouts  3.11 us (6%)
  between operations  0.64 us (1%)
    pallas_call x1, Pallas kernels, per_device(): pl.pallas_call(functools.partial(kernel, (n_sec, n_dp, rows, cols, expert...  47.1 us
    unnamed x2, local copies, waits for them, and re-layouts  3.11 us

profile of v2, /device:TPU:0, one launch (start us, length us, event | category | flops | bytes accessed | tf_op | source)
XLA Modules:
  0.0 50.9 jit_solution(5821723256393472411)
XLA Ops:
  0.6 47.1 %shard_map.95 = (bf16[8,1536]{1,0:T(8,128)(2,1)}, bf16[1,128,1536]{2,1,0:T(8,128)(2,1)}) custom-call(bf16[8,1536]{1,0:T(8,128)(2,1)} %tokens_hbm.1, s32[2,8]{1,0:T(2,128)} %bitcast.3, bf16[8,6144]{1,0:T(8,128)(2,1)} %bitcast.2, bf16[1,6144,4096]{2,1,0:T(8,128)(2,1)} %up_hbm.1, bf16[1,4096,6144]{2,1,0:T(8,128)(2,1)} %down_hbm.1, bf16[1,128,1536]{2,1,0:T(8,128)(2,1)} %q_hbm.1, ...), custom_call_target="tpu_custom_call" | custom-call | tf_op jit(solution)/shard_map/pallas_call | solution.py:325
  47.8 1.3 %copy.12 = bf16[8,1536]{1,0:T(8,128)(2,1)} copy(bf16[8,1536]{1,0:T(8,128)(2,1)} %get-tuple-element.4) | data formatting | bytes 49152
  49.1 1.8 %copy.13 = bf16[1,128,1536]{2,1,0:T(8,128)(2,1)} copy(bf16[1,128,1536]{2,1,0:T(8,128)(2,1)} %get-tuple-element.5) | data formatting | bytes 786432
